TPU v7x, 32 devices: a whole 2x2x4 slice. The times are simulated.
32 devices in a mesh: grp: 4 (over x, core), row: 4 (over z), col: 2 (over y).
Axes of the slice: x: 2, y: 2, z: 4, core: 2. Of those that a mesh axis runs over, the one named last changes fastest.
Arguments:
- fields: bfloat16 [4, 4, 192, 1536], P('grp', None, 'row', 'col'), may hold values from -12 to 12
- offset: int32 [1], replicated, may hold values from 0 to 191
- level_index: int32 [4], replicated, may hold values from 0 to 3, each once
- nudge_rate: float32 [4], replicated, may hold values from 0.2 to 0.9
- driving: float32 [4, 64, 64], replicated, may hold values from -4 to 4
Outputs:
- nudged: bfloat16 [4, 4, 192, 1536], P('grp', None, 'row', 'col')
Inputs may be any that keep to these rules, and one draw needn't show every extreme that they name: `offset`: the footprint covers a third of the parent rows from there on, wrapping around the periodic domain. `level_index`: each parent level is fed by exactly one child level.
All inputs are finite; a program needn't handle non-finite values.
Results may differ from a plain program's by a relative error of at most 0.0034.
Values may be sent and summed in bfloat16 or wider, within the bound.
No kernel may reach another device: no remote copies, remote signals or barrier semaphores. Data moves between devices by JAX's collectives and lax.ppermute only.
A program may use at most 64 MiB of HBM per device.

v0:
```python
import math
import jax
import jax.numpy as jnp
from jax import lax
from jax.sharding import PartitionSpec as P

MAX_WAVE = 32


def from_root(block, axis, source):
    block = jnp.where(lax.axis_index(axis) == source, block, jnp.zeros_like(block))
    return lax.psum(block, axis)


def fourier_table(positions, cell_count, max_order):
    orders = jnp.arange(1, max_order + 1, dtype=jnp.int32)
    period = 3 * cell_count
    phase_index = positions[:, None] * orders[None, :] % period
    angles = phase_index.astype(jnp.float32) * jnp.float32(2.0 * math.pi / period)
    wave_scale = jnp.float32(math.sqrt(2.0 / cell_count))
    constant = jnp.full((positions.shape[0], 1), 1.0 / math.sqrt(cell_count), jnp.float32)
    return jnp.concatenate(
        [constant, wave_scale * jnp.cos(angles), wave_scale * jnp.sin(angles[:, : max_order - 1])],
        axis=1,
    )


def place_rows(carried, block_rows, strip_index):
    height = block_rows.shape[1]
    inside = (strip_index >= 0) & (strip_index < height)
    picked = jnp.take(block_rows, jnp.clip(strip_index, 0, height - 1), axis=1)
    mask_shape = (1, inside.shape[0]) + (1,) * (block_rows.ndim - 2)
    return jnp.where(inside.reshape(mask_shape), picked, carried)


def per_device(fields, offset, level_index, nudge_rate, driving):
    group_id = lax.axis_index("grp")
    row_id = lax.axis_index("row")
    col_id = lax.axis_index("col")
    group_count = lax.axis_size("grp")
    local_slab = fields[0]
    levels, tile_rows, tile_cols = local_slab.shape
    full_rows = lax.axis_size("row") * tile_rows
    full_cols = lax.axis_size("col") * tile_cols
    third_rows = tile_rows // 3
    third_cols = tile_cols // 3
    shift_rows = offset[0]
    is_parent = group_id == group_count - 1
    level_ids = jnp.arange(levels, dtype=jnp.int32)
    inverse = jnp.sum(
        level_ids[:, None] * (level_index[:, None] == level_ids[None, :]).astype(jnp.int32), axis=0
    )
    parent_rows = row_id * tile_rows + jnp.arange(tile_rows, dtype=jnp.int32)
    parent_cols = col_id * tile_cols + jnp.arange(tile_cols, dtype=jnp.int32)
    strip_index = (parent_rows - shift_rows) % full_rows
    covered = strip_index < full_rows // 3
    row_table = fourier_table(3 * parent_rows, full_rows, MAX_WAVE)
    col_table = fourier_table(3 * parent_cols, full_cols, MAX_WAVE)
    row_half = lax.optimization_barrier(row_table.astype(jnp.bfloat16))
    row_rounded = row_half.astype(jnp.float32)
    col_rounded = col_table.astype(jnp.bfloat16)
    block_sums = jnp.sum(
        local_slab.reshape(levels, third_rows, 3, third_cols, 3), axis=(2, 4), dtype=jnp.float32
    )
    averaged = (block_sums / 9.0).astype(jnp.bfloat16)
    by_parent = jnp.take(averaged, inverse, axis=0)
    empty_tile = jnp.zeros((levels, tile_rows, third_cols), jnp.bfloat16)
    placed = place_rows(
        empty_tile, lax.all_gather(by_parent, "row", axis=1, tiled=True), strip_index
    )
    thirds = lax.all_gather(placed[:, :, None, :], "grp", axis=2, tiled=True)
    arrived = thirds[:, :, : group_count - 1, :].reshape(levels, tile_rows, tile_cols)
    fed_tile = jnp.where(covered[None, :, None], arrived, local_slab)
    projected = jnp.einsum("lrc,cm->lrm", fed_tile, col_rounded, preferred_element_type=jnp.float32)
    partial_sums = jnp.einsum(
        "rn,lrm->lnm", row_rounded, projected, precision=lax.Precision.HIGHEST
    )
    summed = lax.psum(partial_sums, ("row", "col"))
    coeffs = from_root(summed, "grp", group_count - 1)
    amplitude = math.sqrt(full_rows * full_cols) / (2 * MAX_WAVE)
    deficit = amplitude * driving - coeffs
    child_rows = (3 * shift_rows + parent_rows - 1) % (3 * full_rows)
    child_cols = (
        (3 * col_id + group_id) * tile_cols + jnp.arange(tile_cols, dtype=jnp.int32) - 1
    ) % (3 * full_cols)
    rows_used = jnp.where(is_parent, row_table, fourier_table(child_rows, full_rows, MAX_WAVE))
    cols_used = jnp.where(is_parent, col_table, fourier_table(child_cols, full_cols, MAX_WAVE))
    level_deficit = jnp.where(is_parent, deficit, jnp.take(deficit, level_index, axis=0))
    level_rate = jnp.where(is_parent, nudge_rate, jnp.take(nudge_rate, level_index, axis=0))
    base_tile = jnp.where(is_parent, fed_tile, local_slab)
    spread_cols = jnp.einsum(
        "lnm,cm->lnc", level_deficit, cols_used, precision=lax.Precision.HIGHEST
    )
    increment = jnp.einsum("rn,lnc->lrc", rows_used, spread_cols, precision=lax.Precision.HIGHEST)
    result = (base_tile.astype(jnp.float32) + level_rate[:, None, None] * increment).astype(
        jnp.bfloat16
    )
    return result[None]


def solution(mesh):
    placed = (P("grp", None, "row", "col"), P(), P(), P(), P())
    return jax.shard_map(
        per_device,
        mesh=mesh,
        in_specs=placed,
        out_specs=P("grp", None, "row", "col"),
        check_vma=False,
    )
```

profile of v0, /device:TPU:0, one launch (start us, length us, event | category | flops | bytes accessed | tf_op | source)
XLA Modules:
  0.0 187.4 jit_solution(7154075441931077724)
XLA Ops:
  6.5 0.0 all-reduce.3.cloned.1.call-start
  6.5 0.7 select_reduce_fusion
  8.0 0.0 copy-start.1
  8.0 0.0 copy-start.3
  8.0 0.0 copy-start
  8.0 0.0 copy-start.2
  8.1 25.9 %reshape.136 = f32[4,16,3,256,3]{4,3,2,1,0:T(8,128)} reshape(bf16[1,4,48,768]{3,2,1,0:T(8,128)(2,1)} %param.5) | data formatting | bytes 884736 | tf_op jit(solution)/shard_map/convert_element_type | solution.py:62
  34.0 11.8 %reduce_sum.21 = f32[4,16,256]{2,1,0:T(8,128)S(1)} reduce(f32[4,16,3,256,3]{4,3,2,1,0:T(8,128)} %reshape.136, f32[]{:T(128)} %constant.140.clone.1), dimensions={2,4}, to_apply=%region_1.2 | reduce | flops 131072 | bytes 655364 | tf_op jit(solution)/shard_map/reduce_sum | solution.py:62
  45.8 0.5 gather_fusion
  46.3 0.1 broadcast_select_fusion.1
  46.4 15.1 %all_gather.6 = bf16[4,64,256]{2,1,0:T(8,128)(2,1)S(1)} all-gather(bf16[4,16,256]{2,1,0:T(8,128)(2,1)S(1)} %broadcast_select_fusion.1), channel_id=1, replica_groups=mesh['grp'=4,'row'=4,'col'=2] {'row'}, dimensions={1}, use_global_device_ids=true | all-gather | bytes 163840 | tf_op jit(solution)/shard_map/all_gather | solution.py:69
  61.5 0.1 copy.20
  61.6 0.7 gather_fusion.1
  62.3 0.1 fusion.24
  62.4 6.5 %all_gather.7 = bf16[4,48,4,256]{3,1,0,2:T(8,128)(2,1)S(1)} all-gather(bf16[4,48,1,256]{3,1,0,2:T(8,128)(2,1)S(1)} %fusion.24), channel_id=1, replica_groups=mesh['grp'=4,'row'=4,'col'=2] {'grp'}, dimensions={2}, use_global_device_ids=true | all-gather | bytes 491520 | tf_op jit(solution)/shard_map/all_gather | solution.py:71
  68.9 0.8 cosine_multiply_fusion.1
  69.7 0.3 fusion.21
  70.1 0.3 cosine_multiply_fusion.2
  70.4 0.1 fusion.40
  70.5 0.1 fusion.55
  70.6 0.0 copy-done.1
  70.6 0.3 fusion.13
  70.9 1.0 convolution_bitcast_fusion
  71.9 0.0 all-reduce.3.cloned.1.call-update
  71.9 0.0 all-reduce.5.cloned.1.call-start
  71.9 0.0 copy-done.3
  72.0 0.3 fusion.20
  72.3 0.1 fusion.39
  72.4 0.0 copy-done
  72.4 0.6 gather_fusion.2
  73.1 70.4 %all-reduce.3.cloned.1.call-done = f32[4,64,64]{1,2,0:T(8,128)} async-done(((f32[4,64,64]{1,2,0:T(8,128)}), f32[4,64,64]{1,2,0:T(8,128)}) %all-reduce.3.cloned.1.call-update) | async-done | bytes 65552 | tf_op jit(solution)/shard_map/psum | solution.py:78
  143.4 0.7 broadcast_select_fusion
  144.1 0.0 all-reduce.5.cloned.1.call-update
  144.1 0.0 copy-done.2
  144.1 0.1 copy.23
  144.2 32.4 %all-reduce.5.cloned.1.call-done = f32[4,64,64]{1,2,0:T(8,128)} async-done(((f32[4,64,64]{1,2,0:T(8,128)}), f32[4,64,64]{1,2,0:T(8,128)}) %all-reduce.5.cloned.1.call-update) | async-done | bytes 65552 | tf_op jit(solution)/shard_map/psum | solution.py:12
  176.6 0.9 multiply_subtract_fusion
  177.6 0.6 gather_fusion.3
  178.1 0.9 fusion.5
  179.1 1.5 fusion.3
  (19 shorter events, 0.2 us)
Async XLA Ops:
  6.5 136.9 %all-reduce.3.cloned.1.call-start = ((), (), s32[]{:S(2)}) async-start(), calls=%async_computation | async-start | bytes 262144 | tf_op jit(solution)/shard_map/psum | solution.py:78
  8.0 62.6 %copy-start.1 = (bf16[1,4,48,768]{3,2,1,0:T(8,128)(2,1)S(1)}, bf16[1,4,48,768]{3,2,1,0:T(8,128)(2,1)}, u32[]{:S(2)}) copy-start(bf16[1,4,48,768]{3,2,1,0:T(8,128)(2,1)} %param.5) | copy-start | bytes 884740
  8.0 63.9 %copy-start.3 = (s32[4]{0:T(128)S(1)}, s32[4]{0:T(128)}, u32[]{:S(2)}) copy-start(s32[4]{0:T(128)} %param.7) | copy-start | bytes 52
  8.0 64.4 %copy-start = (f32[4]{0:T(128)S(1)}, f32[4]{0:T(128)}, u32[]{:S(2)}) copy-start(f32[4]{0:T(128)} %param.8) | copy-start | bytes 52
  8.0 136.1 %copy-start.2 = (f32[4,64,64]{2,1,0:T(8,128)S(1)}, f32[4,64,64]{2,1,0:T(8,128)}, u32[]{:S(2)}) copy-start(f32[4,64,64]{2,1,0:T(8,128)} %param.9) | copy-start | bytes 196612
  71.9 104.8 %all-reduce.5.cloned.1.call-start = ((), (), s32[]{:S(2)}) async-start(), calls=%async_computation.1 | async-start | bytes 262144 | tf_op jit(solution)/shard_map/psum | solution.py:12
Sparse Core Ops, SparseCore 0:
  72.0 71.3 all-reduce.2
  145.7 30.8 all-reduce.4
where the time goes:
time: 188 us; the launch traced here: 187 us
  waiting for transfers between devices  103 us (55%)
  local copies, waits for them, and re-layouts  28.6 us (15%)
  blocking collectives  21.5 us (11%)
  other arithmetic  16.5 us (9%)
  between operations  14.3 us (8%)
  matrix products  3.65 us (2%)
    psum x1, waiting for transfers between devices, per_device(): summed = lax.psum(partial_sums, ('row', 'col'))  70.4 us
    psum x1, waiting for transfers between devices, from_root(): return lax.psum(block, axis)  32.4 us
    convert_element_type x1, local copies, waits for them, and re-layouts, per_device(): jnp.sum(local_slab.reshape(levels, third_rows, 3, third_cols, 3), axis=(2...  25.9 us
    all_gather x1, blocking collectives, per_device(): lax.all_gather(by_parent, 'row', axis=1, tiled=True)  15.1 us
    reduce_sum x1, other arithmetic, per_device(): jnp.sum(local_slab.reshape(levels, third_rows, 3, third_cols, 3), axis=(2...  11.8 us
    all_gather x1, blocking collectives, per_device(): thirds = lax.all_gather(placed[:, :, None, :], 'grp', axis=2, tiled=True)  6.46 us
  transfers between devices with their start and end apart: 2, of which 2 were waited for; matrix products, arithmetic and copies ran while one was open for 1% of the time, Pallas kernels for 0%

commit v1 on v0

--- a/solution.py
+++ b/solution.py
@@ -5,6 +5,27 @@
 from jax.sharding import PartitionSpec as P
 
 MAX_WAVE = 32
+
+
+def gather_around(x, axis, dim):
+    size, place, width = (lax.axis_size(axis), lax.axis_index(axis), x.shape[dim])
+    upward = [(i, (i + 1) % size) for i in range(size)]
+    downward = [(i, (i - 1) % size) for i in range(size)]
+    filled = jnp.zeros((*x.shape[:dim], size * width, *x.shape[dim + 1 :]), x.dtype)
+    filled = lax.dynamic_update_slice_in_dim(filled, x, place * width, axis=dim)
+    from_left = from_right = x
+    halfway = size // 2
+    for hop in range(1, halfway + 1):
+        from_left = lax.ppermute(from_left, axis, upward)
+        filled = lax.dynamic_update_slice_in_dim(
+            filled, from_left, (place - hop) % size * width, axis=dim
+        )
+        if hop < size - halfway:
+            from_right = lax.ppermute(from_right, axis, downward)
+            filled = lax.dynamic_update_slice_in_dim(
+                filled, from_right, (place + hop) % size * width, axis=dim
+            )
+    return filled
 
 
 def from_root(block, axis, source):
@@ -65,9 +86,7 @@
     averaged = (block_sums / 9.0).astype(jnp.bfloat16)
     by_parent = jnp.take(averaged, inverse, axis=0)
     empty_tile = jnp.zeros((levels, tile_rows, third_cols), jnp.bfloat16)
-    placed = place_rows(
-        empty_tile, lax.all_gather(by_parent, "row", axis=1, tiled=True), strip_index
-    )
+    placed = place_rows(empty_tile, gather_around(by_parent, "row", 1), strip_index)
     thirds = lax.all_gather(placed[:, :, None, :], "grp", axis=2, tiled=True)
     arrived = thirds[:, :, : group_count - 1, :].reshape(levels, tile_rows, tile_cols)
     fed_tile = jnp.where(covered[None, :, None], arrived, local_slab)

time: 188 us -> 182 us (0.968)
  blocking collectives: 21.5 us -> 6.62 us
  starting transfers between devices: 0.04 us -> 5.21 us
  waiting for transfers between devices: 103 us -> 106 us
    all_gather x1 -> x0, blocking collectives: 15.1 us -> none  [per_device(): lax.all_gather(by_parent, 'row', axis=1, tiled=True)]
    ppermute x0 -> x3, waiting for transfers between devices: none -> 5.62 us  [the longest x2 5.62 us: gather_around(): from_left = lax.ppermute(from_left, axis, upward)]
    ppermute x0 -> x3, starting transfers between devices: none -> 5.17 us  [the longest x2 3.09 us: gather_around(): from_left = lax.ppermute(from_left, axis, upward)]
    psum x1, waiting for transfers between devices: 70.4 us -> 68.4 us  [per_device(): summed = lax.psum(partial_sums, ('row', 'col'))]
  transfers between devices with their start and end apart: 2 -> 5, of which waited for: 2 -> 3; matrix products, arithmetic and copies ran while one was open for 1% -> 2% of each run, Pallas kernels for 0% -> 0%
where the time goes in v1:
time: 182 us; the launch traced here: 181 us
  waiting for transfers between devices  106 us (58%)
  local copies, waits for them, and re-layouts  28.7 us (16%)
  other arithmetic  16.5 us (9%)
  between operations  14.4 us (8%)
  blocking collectives  6.62 us (4%)
  starting transfers between devices  5.21 us (3%)
  matrix products  3.67 us (2%)
    psum x1, waiting for transfers between devices, per_device(): summed = lax.psum(partial_sums, ('row', 'col'))  68.4 us
    psum x1, waiting for transfers between devices, from_root(): return lax.psum(block, axis)  32.4 us
    convert_element_type x1, local copies, waits for them, and re-layouts, per_device(): jnp.sum(local_slab.reshape(levels, third_rows, 3, third_cols, 3), axis=(2...  25.9 us
    reduce_sum x1, other arithmetic, per_device(): jnp.sum(local_slab.reshape(levels, third_rows, 3, third_cols, 3), axis=(2...  11.8 us
    all_gather x1, blocking collectives, per_device(): thirds = lax.all_gather(placed[:, :, None, :], 'grp', axis=2, tiled=True)  6.62 us
    ppermute x2, waiting for transfers between devices, gather_around(): from_left = lax.ppermute(from_left, axis, upward)  5.62 us
  transfers between devices with their start and end apart: 5, of which 3 were waited for; matrix products, arithmetic and copies ran while one was open for 2% of the time, Pallas kernels for 0%

profile of v1, /device:TPU:0, one launch (start us, length us, event | category | flops | bytes accessed | tf_op | source)
XLA Modules:
  0.0 181.5 jit_solution(12510465668985892553)
XLA Ops:
  6.5 0.0 all-reduce.3.cloned.1.call-start
  6.5 0.7 select_reduce_fusion
  7.3 0.0 copy-start.3
  7.3 0.0 copy-start
  7.3 0.0 copy-start.1
  7.3 0.0 copy-start.2
  7.4 25.9 %reshape.136 = f32[4,16,3,256,3]{4,3,2,1,0:T(8,128)} reshape(bf16[1,4,48,768]{3,2,1,0:T(8,128)(2,1)} %param.5) | data formatting | bytes 884736 | tf_op jit(solution)/shard_map/convert_element_type | solution.py:83
  33.3 11.8 %reduce_sum.21 = f32[4,16,256]{2,1,0:T(8,128)S(1)} reduce(f32[4,16,3,256,3]{4,3,2,1,0:T(8,128)} %reshape.136, f32[]{:T(128)} %constant.166.clone.1), dimensions={2,4}, to_apply=%region_1.2 | reduce | flops 131072 | bytes 655364 | tf_op jit(solution)/shard_map/reduce_sum | solution.py:83
  45.1 0.5 gather_fusion
  45.7 0.1 broadcast_select_fusion.1
  45.7 3.1 %collective-permute-start = (bf16[4,16,256]{2,1,0:T(8,128)(2,1)S(1)}, bf16[4,16,256]{2,1,0:T(8,128)(2,1)S(1)}, u32[]{:S(2)}, u32[]{:S(2)}) collective-permute-start(bf16[4,16,256]{2,1,0:T(8,128)(2,1)S(1)} %broadcast_select_fusion.1), channel_id=1, source_target_pairs={{0,2},{2,4},{4,6},{6,0},{1,3},{3,5},{5,7},{7,1},{8,10},{10,12},{12... | collective-permute-start | bytes 98312 | tf_op jit(solution)/shard_map/ppermute | solution.py:19
  48.8 2.1 %collective-permute-start.1 = (bf16[4,16,256]{2,1,0:T(8,128)(2,1)S(1)}, bf16[4,16,256]{2,1,0:T(8,128)(2,1)S(1)}, u32[]{:S(2)}, u32[]{:S(2)}) collective-permute-start(bf16[4,16,256]{2,1,0:T(8,128)(2,1)S(1)} %broadcast_select_fusion.1), channel_id=1, source_target_pairs={{0,6},{2,0},{4,2},{6,4},{1,7},{3,1},{5,3},{7,5},{8,14},{10,8},{12,... | collective-permute-start | bytes 98312 | tf_op jit(solution)/shard_map/ppermute | solution.py:24
  50.9 0.0 copy-done.3
  51.6 0.8 cosine_multiply_fusion.1
  52.4 0.3 fusion.21
  52.8 0.3 cosine_multiply_fusion.2
  53.1 0.1 fusion.40
  53.2 0.3 fusion.20
  53.5 0.1 fusion.39
  53.7 0.1 fusion.55
  53.9 0.0 copy-done
  53.9 0.6 gather_fusion.2
  54.6 0.0 collective-permute-done
  54.6 0.0 collective-permute-start.2
  54.7 0.0 collective-permute-done.1
  54.7 5.6 %collective-permute-done.2 = bf16[4,16,256]{2,1,0:T(8,128)(2,1)S(1)} collective-permute-done((bf16[4,16,256]{2,1,0:T(8,128)(2,1)S(1)}, bf16[4,16,256]{2,1,0:T(8,128)(2,1)S(1)}, u32[]{:S(2)}, u32[]{:S(2)}) %collective-permute-start.2) | collective-permute-done | bytes 32800 | tf_op jit(solution)/shard_map/ppermute | solution.py:19
  60.3 0.7 gather_fusion.1
  61.0 0.1 fusion.24
  61.1 6.6 %all_gather.3 = bf16[4,48,4,256]{3,1,0,2:T(8,128)(2,1)S(1)} all-gather(bf16[4,48,1,256]{3,1,0,2:T(8,128)(2,1)S(1)} %fusion.24), channel_id=1, replica_groups=mesh['grp'=4,'row'=4,'col'=2] {'grp'}, dimensions={2}, use_global_device_ids=true | all-gather | bytes 491520 | tf_op jit(solution)/shard_map/all_gather | solution.py:90
  67.8 0.0 copy-done.1
  67.8 0.3 fusion.13
  68.1 1.0 convolution_bitcast_fusion
  69.0 0.0 all-reduce.3.cloned.1.call-update
  69.1 0.0 all-reduce.5.cloned.1.call-start
  69.1 68.4 %all-reduce.3.cloned.1.call-done = f32[4,64,64]{1,2,0:T(8,128)} async-done(((f32[4,64,64]{1,2,0:T(8,128)}), f32[4,64,64]{1,2,0:T(8,128)}) %all-reduce.3.cloned.1.call-update) | async-done | bytes 65552 | tf_op jit(solution)/shard_map/psum | solution.py:97
  137.5 0.7 broadcast_select_fusion
  138.2 0.0 all-reduce.5.cloned.1.call-update
  138.2 0.0 copy-done.2
  138.2 0.1 copy.32
  138.3 32.4 %all-reduce.5.cloned.1.call-done = f32[4,64,64]{1,2,0:T(8,128)} async-done(((f32[4,64,64]{1,2,0:T(8,128)}), f32[4,64,64]{1,2,0:T(8,128)}) %all-reduce.5.cloned.1.call-update) | async-done | bytes 65552 | tf_op jit(solution)/shard_map/psum | solution.py:33
  170.7 0.9 multiply_subtract_fusion
  171.7 0.6 gather_fusion.3
  172.2 0.9 fusion.5
  173.2 1.5 fusion.3
  (24 shorter events, 0.4 us)
Async XLA Ops:
  6.5 131.0 %all-reduce.3.cloned.1.call-start = ((), (), s32[]{:S(2)}) async-start(), calls=%async_computation | async-start | bytes 262144 | tf_op jit(solution)/shard_map/psum | solution.py:97
  7.3 43.6 %copy-start.3 = (s32[4]{0:T(128)S(1)}, s32[4]{0:T(128)}, u32[]{:S(2)}) copy-start(s32[4]{0:T(128)} %param.7) | copy-start | bytes 52
  7.3 46.6 %copy-start = (f32[4]{0:T(128)S(1)}, f32[4]{0:T(128)}, u32[]{:S(2)}) copy-start(f32[4]{0:T(128)} %param.8) | copy-start | bytes 52
  7.3 60.4 %copy-start.1 = (bf16[1,4,48,768]{3,2,1,0:T(8,128)(2,1)S(1)}, bf16[1,4,48,768]{3,2,1,0:T(8,128)(2,1)}, u32[]{:S(2)}) copy-start(bf16[1,4,48,768]{3,2,1,0:T(8,128)(2,1)} %param.5) | copy-start | bytes 884740
  7.3 130.9 %copy-start.2 = (f32[4,64,64]{2,1,0:T(8,128)S(1)}, f32[4,64,64]{2,1,0:T(8,128)}, u32[]{:S(2)}) copy-start(f32[4,64,64]{2,1,0:T(8,128)} %param.9) | copy-start | bytes 196612
  45.7 8.8 %collective-permute-start = (bf16[4,16,256]{2,1,0:T(8,128)(2,1)S(1)}, bf16[4,16,256]{2,1,0:T(8,128)(2,1)S(1)}, u32[]{:S(2)}, u32[]{:S(2)}) collective-permute-start(bf16[4,16,256]{2,1,0:T(8,128)(2,1)S(1)} %broadcast_select_fusion.1), channel_id=1, source_target_pairs={{0,2},{2,4},{4,6},{6,0},{1,3},{3,5},{5,7},{7,1},{8,10},{10,12},{12... | collective-permute-start | bytes 98312 | tf_op jit(solution)/shard_map/ppermute | solution.py:19
  48.8 5.9 %collective-permute-start.1 = (bf16[4,16,256]{2,1,0:T(8,128)(2,1)S(1)}, bf16[4,16,256]{2,1,0:T(8,128)(2,1)S(1)}, u32[]{:S(2)}, u32[]{:S(2)}) collective-permute-start(bf16[4,16,256]{2,1,0:T(8,128)(2,1)S(1)} %broadcast_select_fusion.1), channel_id=1, source_target_pairs={{0,6},{2,0},{4,2},{6,4},{1,7},{3,1},{5,3},{7,5},{8,14},{10,8},{12,... | collective-permute-start | bytes 98312 | tf_op jit(solution)/shard_map/ppermute | solution.py:24
  54.6 5.7 %collective-permute-start.2 = (bf16[4,16,256]{2,1,0:T(8,128)(2,1)S(1)}, bf16[4,16,256]{2,1,0:T(8,128)(2,1)S(1)}, u32[]{:S(2)}, u32[]{:S(2)}) collective-permute-start(bf16[4,16,256]{2,1,0:T(8,128)(2,1)S(1)} %collective-permute-done), channel_id=1, source_target_pairs={{0,2},{2,4},{4,6},{6,0},{1,3},{3,5},{5,7},{7,1},{8,10},{10,12},{12... | collective-permute-start | bytes 98312 | tf_op jit(solution)/shard_map/ppermute | solution.py:19
  69.1 101.7 %all-reduce.5.cloned.1.call-start = ((), (), s32[]{:S(2)}) async-start(), calls=%async_computation.1 | async-start | bytes 262144 | tf_op jit(solution)/shard_map/psum | solution.py:33
Sparse Core Ops, SparseCore 0:
  69.2 68.2 all-reduce.2
  139.8 30.8 all-reduce.4
